TPU v7x, 32 devices: a whole 2x2x4 slice. The times are simulated.
32 devices in a mesh: tensor: 2 (over y), dp: 4 (over x, core), seq: 4 (over z).
Axes of the slice: x: 2, y: 2, z: 4, core: 2. Of those that a mesh axis runs over, the one named last changes fastest.
Arguments:
- tokens: bfloat16 [8, 1024, 2048], P('dp', 'seq'), may hold values from -6 to 6
- ln1_gain: bfloat16 [2048], P(('dp', 'seq')), may hold values from 0.5 to 1.5
- ln1_bias: bfloat16 [2048], P(('dp', 'seq')), may hold values from -3 to 3
- ln2_gain: bfloat16 [2048], P(('dp', 'seq')), may hold values from 0.5 to 1.5
- ln2_bias: bfloat16 [2048], P(('dp', 'seq')), may hold values from -3 to 3
- w_query: bfloat16 [2048, 2048], P(('dp', 'seq'), 'tensor'), may hold values from -0.125 to 0.125
- w_key: bfloat16 [2048, 2048], P(('dp', 'seq'), 'tensor'), may hold values from -0.125 to 0.125
- w_value: bfloat16 [2048, 4096], P(('dp', 'seq'), 'tensor'), may hold values from -0.125 to 0.125
- w_swish: bfloat16 [2048, 4096], P(('dp', 'seq'), 'tensor'), may hold values from -0.125 to 0.125
- w_out: bfloat16 [4096, 2048], P('tensor', ('dp', 'seq')), may hold values from -0.1875 to 0.1875
- w_gate: bfloat16 [2048, 4096], P(('dp', 'seq'), 'tensor'), may hold values from -0.125 to 0.125
- w_up: bfloat16 [2048, 4096], P(('dp', 'seq'), 'tensor'), may hold values from -0.125 to 0.125
- w_down: bfloat16 [4096, 2048], P('tensor', ('dp', 'seq')), may hold values from -0.09375 to 0.09375
- decay_rate: float32 [8], P('tensor'), may hold values from 0 to 1, as said below
- cotangent: bfloat16 [8, 1024, 2048], P('dp', 'seq'), may hold values from -6 to 6
Outputs:
- mixed_out: bfloat16 [8, 1024, 2048], P('dp', 'seq')
- input_grad: float32 [8, 1024, 2048], P('dp', 'seq')
- ln1_gain_grad: float32 [2048], P(('dp', 'seq'))
- ln1_bias_grad: float32 [2048], P(('dp', 'seq'))
- ln2_gain_grad: float32 [2048], P(('dp', 'seq'))
- ln2_bias_grad: float32 [2048], P(('dp', 'seq'))
- w_query_grad: float32 [2048, 2048], P(('dp', 'seq'), 'tensor')
- w_key_grad: float32 [2048, 2048], P(('dp', 'seq'), 'tensor')
- w_value_grad: float32 [2048, 4096], P(('dp', 'seq'), 'tensor')
- w_swish_grad: float32 [2048, 4096], P(('dp', 'seq'), 'tensor')
- w_out_grad: float32 [4096, 2048], P('tensor', ('dp', 'seq'))
- w_gate_grad: float32 [2048, 4096], P(('dp', 'seq'), 'tensor')
- w_up_grad: float32 [2048, 4096], P(('dp', 'seq'), 'tensor')
- w_down_grad: float32 [4096, 2048], P('tensor', ('dp', 'seq'))
Inputs may be any that keep to these rules, and one draw needn't show every extreme that they name: `decay_rate`: each head's rate lies between 0.3 / 1024 and 1 / 30.
All inputs are finite; a program needn't handle non-finite values.
Results may differ from a plain program's by a relative error of at most 0.014.
Values may be sent and summed in bfloat16 or wider, within the bound.
A program may use at most 256 MiB of HBM per device.

v0:
```python
import jax
import jax.numpy as jnp
from jax import lax
from jax.sharding import PartitionSpec as P

KD = 256
VH = 512
eps = 1e-05
highest_precision = lax.Precision.HIGHEST


def passed_along(x, axis, by):
    count = lax.axis_size(axis)
    pairs = [(i, i + by) for i in range(count) if 0 <= i + by < count]
    return lax.ppermute(x, axis, pairs)


def normalize(values):
    centred = values - jnp.mean(values, axis=-1, keepdims=True)
    spread = jnp.mean(centred * centred, axis=-1, keepdims=True)
    scaling = lax.rsqrt(spread + eps)
    return (centred * scaling, scaling)


def norm_back(grad_normed, normed, scaling):
    first_mean = jnp.mean(grad_normed, axis=-1, keepdims=True)
    second_mean = jnp.mean(grad_normed * normed, axis=-1, keepdims=True)
    return scaling * (grad_normed - first_mean - normed * second_mean)


def turn_angles(positions, half_width):
    frequency = 10000.0 ** (-jnp.arange(half_width, dtype=jnp.float32) / max(half_width - 1, 1))
    angles = positions[:, None] * frequency[None, :]
    return (jnp.cos(angles)[:, None, :], jnp.sin(angles)[:, None, :])


def rotate(values, cosine, sine_table):
    half_width = values.shape[-1] // 2
    first_half = values[..., :half_width]
    second_half = values[..., half_width:]
    return jnp.concatenate(
        [
            first_half * cosine - second_half * sine_table,
            second_half * cosine + first_half * sine_table,
        ],
        axis=-1,
    )


def decay_tables(decay_rate, block):
    places = jnp.arange(block, dtype=jnp.float32)
    distance = places[:, None] - places[None, :]
    inside = jnp.where(
        distance[None] >= 0.0,
        jnp.exp(-decay_rate[:, None, None] * jnp.maximum(distance, 0.0)[None]),
        0.0,
    )
    query_decay_factor = jnp.exp(-decay_rate[None, :] * (places[:, None] + 1.0))[..., None]
    key_decay_factor = jnp.exp(-decay_rate[None, :] * (block - 1.0 - places[:, None]))[..., None]
    block_decay_factor = jnp.exp(-decay_rate * block)[:, None, None]
    return (inside, query_decay_factor, key_decay_factor, block_decay_factor)


def matmul(left, right):
    return jnp.dot(left, right, preferred_element_type=jnp.float32)


def on_device(
    tokens,
    ln1_gain,
    ln1_bias,
    ln2_gain,
    ln2_bias,
    w_query,
    w_key,
    w_value,
    w_swish,
    w_out,
    w_gate,
    w_up,
    w_down,
    decay_rate,
    cotangent,
):
    gathered = (
        lax.all_gather(ln1_gain, ("dp", "seq"), axis=0, tiled=True),
        lax.all_gather(ln1_bias, ("dp", "seq"), axis=0, tiled=True),
        lax.all_gather(ln2_gain, ("dp", "seq"), axis=0, tiled=True),
        lax.all_gather(ln2_bias, ("dp", "seq"), axis=0, tiled=True),
        lax.all_gather(w_query, ("dp", "seq"), axis=0, tiled=True),
        lax.all_gather(w_key, ("dp", "seq"), axis=0, tiled=True),
        lax.all_gather(w_value, ("dp", "seq"), axis=0, tiled=True),
        lax.all_gather(w_swish, ("dp", "seq"), axis=0, tiled=True),
        lax.all_gather(w_gate, ("dp", "seq"), axis=0, tiled=True),
        lax.all_gather(w_up, ("dp", "seq"), axis=0, tiled=True),
    )
    norm_gain = gathered[0].astype(jnp.float32)
    norm_bias = gathered[1].astype(jnp.float32)
    mlp_gain = gathered[2].astype(jnp.float32)
    mlp_bias = gathered[3].astype(jnp.float32)
    query_full, key_full, value_full, swish_full, gate_full, up_full = gathered[4:]
    out_full, down_full = (
        lax.all_gather(w_out, ("dp", "seq"), axis=1, tiled=True),
        lax.all_gather(w_down, ("dp", "seq"), axis=1, tiled=True),
    )
    seq_count, block, width = tokens.shape
    row_count = seq_count * block
    heads = decay_rate.shape[0]
    inputs = tokens.astype(jnp.float32).reshape(row_count, width)
    normed_one, scale_one = normalize(inputs)
    first = (normed_one * norm_gain + norm_bias).astype(jnp.bfloat16)
    queries = matmul(first, query_full).reshape(seq_count, block, heads, KD)
    keys_lin = matmul(first, key_full).reshape(seq_count, block, heads, KD)
    value_rows = matmul(first, value_full).astype(jnp.bfloat16).reshape(seq_count, block, heads, VH)
    gate_pre = matmul(first, swish_full)
    offset = lax.axis_index("seq") * block
    positions = (offset + jnp.arange(block, dtype=jnp.int32)).astype(jnp.float32)
    cosine, sine_table = turn_angles(positions, KD // 2)
    query_rot = rotate(queries, cosine, sine_table).astype(jnp.bfloat16)
    key_rot = rotate(keys_lin, cosine, sine_table).astype(jnp.bfloat16)
    inside, query_decay_factor, key_decay_factor, block_decay_factor = decay_tables(
        decay_rate, block
    )
    scores = jnp.einsum("snhk,smhk->shnm", query_rot, key_rot, preferred_element_type=jnp.float32)
    weights = (scores * inside).astype(jnp.bfloat16)
    within = jnp.einsum("shnm,smhv->snhv", weights, value_rows, preferred_element_type=jnp.float32)
    query_scaled = query_rot.astype(jnp.float32) * query_decay_factor
    key_scaled = key_rot.astype(jnp.float32) * key_decay_factor
    value_wide = value_rows.astype(jnp.float32)
    local_state = jnp.einsum("smhk,smhv->shkv", key_scaled, value_wide, precision=highest_precision)

    def pass_state(turn, carry):
        incoming = passed_along(carry[1], "seq", 1)
        return (incoming, block_decay_factor * incoming + local_state)

    state_in = lax.fori_loop(
        0, lax.axis_size("seq") - 1, pass_state, (jnp.zeros_like(local_state), local_state)
    )[0]
    cross_block_term = jnp.einsum(
        "snhk,shkv->snhv", query_scaled, state_in, precision=highest_precision
    )
    retained = within + cross_block_term
    group_normed, group_scale = normalize(retained)
    group_flat = group_normed.reshape(row_count, heads * VH)
    gate_act, swish_pull = jax.vjp(jax.nn.silu, gate_pre)
    mixed = (gate_act * group_flat).astype(jnp.bfloat16)
    attention = lax.psum(matmul(mixed, out_full), "tensor")
    hidden_in = inputs + attention
    normed_two, scale_two = normalize(hidden_in)
    second = (normed_two * mlp_gain + mlp_bias).astype(jnp.bfloat16)
    gate_lin = matmul(second, gate_full)
    up_lin = matmul(second, up_full)
    gate_gelu, gelu_pull = jax.vjp(jax.nn.gelu, gate_lin)
    hidden = (gate_gelu * up_lin).astype(jnp.bfloat16)
    feed = lax.psum(matmul(hidden, down_full).astype(jnp.bfloat16), "tensor").astype(jnp.float32)
    mixed_out = (hidden_in + feed).astype(jnp.bfloat16).reshape(seq_count, block, width)
    grad_rows = cotangent.reshape(row_count, width)
    grad_down = jnp.einsum("rf,rd->fd", hidden, grad_rows, preferred_element_type=jnp.float32)
    grad_hidden = jnp.einsum("rd,fd->rf", grad_rows, down_full, preferred_element_type=jnp.float32)
    grad_gate_lin = gelu_pull(grad_hidden * up_lin)[0].astype(jnp.bfloat16)
    grad_up_lin = (grad_hidden * gate_gelu).astype(jnp.bfloat16)
    grad_gate = jnp.einsum("rd,rf->df", second, grad_gate_lin, preferred_element_type=jnp.float32)
    grad_up = jnp.einsum("rd,rf->df", second, grad_up_lin, preferred_element_type=jnp.float32)
    second_part = jnp.einsum(
        "rf,df->rd", grad_gate_lin, gate_full, preferred_element_type=jnp.float32
    )
    second_part = second_part + jnp.einsum(
        "rf,df->rd", grad_up_lin, up_full, preferred_element_type=jnp.float32
    )
    grad_second = lax.psum(second_part, "tensor")
    grad_mlp_gain = jnp.sum(grad_second * normed_two, axis=0)
    grad_mlp_bias = jnp.sum(grad_second, axis=0)
    grad_hidden_in = grad_rows.astype(jnp.float32) + norm_back(
        grad_second * mlp_gain, normed_two, scale_two
    )
    grad_branch = grad_hidden_in.astype(jnp.bfloat16)
    grad_out_w = jnp.einsum("rv,rd->vd", mixed, grad_branch, preferred_element_type=jnp.float32)
    grad_mixed = jnp.einsum("rd,vd->rv", grad_branch, out_full, preferred_element_type=jnp.float32)
    grad_gate_pre = swish_pull(grad_mixed * group_flat)[0].astype(jnp.bfloat16)
    grad_group = (grad_mixed * gate_act).reshape(seq_count, block, heads, VH)
    grad_retained = norm_back(grad_group, group_normed, group_scale).astype(jnp.bfloat16)
    grad_weights = jnp.einsum(
        "snhv,smhv->shnm", grad_retained, value_rows, preferred_element_type=jnp.float32
    )
    grad_scores = (grad_weights * inside).astype(jnp.bfloat16)
    grad_query = jnp.einsum(
        "shnm,smhk->snhk", grad_scores, key_rot, preferred_element_type=jnp.float32
    )
    grad_key = jnp.einsum(
        "shnm,snhk->smhk", grad_scores, query_rot, preferred_element_type=jnp.float32
    )
    grad_value = jnp.einsum(
        "shnm,snhv->smhv", weights, grad_retained, preferred_element_type=jnp.float32
    )
    grad_wide = grad_retained.astype(jnp.float32)
    grad_query = grad_query + query_decay_factor * jnp.einsum(
        "snhv,shkv->snhk", grad_wide, state_in, precision=highest_precision
    )
    local_grad = jnp.einsum("snhk,snhv->shkv", query_scaled, grad_wide, precision=highest_precision)

    def pass_grad(turn, carry):
        incoming = passed_along(carry[1], "seq", -1)
        return (incoming, block_decay_factor * incoming + local_grad)

    state_grad = lax.fori_loop(
        0, lax.axis_size("seq") - 1, pass_grad, (jnp.zeros_like(local_grad), local_grad)
    )[0]
    grad_key = grad_key + key_decay_factor * jnp.einsum(
        "smhv,shkv->smhk", value_wide, state_grad, precision=highest_precision
    )
    grad_value = grad_value + jnp.einsum(
        "smhk,shkv->smhv", key_scaled, state_grad, precision=highest_precision
    )
    grad_query_pre = (
        rotate(grad_query, cosine, -sine_table).reshape(row_count, heads * KD).astype(jnp.bfloat16)
    )
    grad_key_pre = (
        rotate(grad_key, cosine, -sine_table).reshape(row_count, heads * KD).astype(jnp.bfloat16)
    )
    grad_value_pre = grad_value.reshape(row_count, heads * VH).astype(jnp.bfloat16)
    grad_wq = jnp.einsum("rd,rk->dk", first, grad_query_pre, preferred_element_type=jnp.float32)
    grad_wk = jnp.einsum("rd,rk->dk", first, grad_key_pre, preferred_element_type=jnp.float32)
    grad_wv = jnp.einsum("rd,rk->dk", first, grad_value_pre, preferred_element_type=jnp.float32)
    grad_ws = jnp.einsum("rd,rk->dk", first, grad_gate_pre, preferred_element_type=jnp.float32)
    first_part = jnp.einsum(
        "rk,dk->rd", grad_query_pre, query_full, preferred_element_type=jnp.float32
    )
    first_part = first_part + jnp.einsum(
        "rk,dk->rd", grad_key_pre, key_full, preferred_element_type=jnp.float32
    )
    first_part = first_part + jnp.einsum(
        "rk,dk->rd", grad_value_pre, value_full, preferred_element_type=jnp.float32
    )
    first_part = first_part + jnp.einsum(
        "rk,dk->rd", grad_gate_pre, swish_full, preferred_element_type=jnp.float32
    )
    grad_first = lax.psum(first_part, "tensor")
    grad_norm_gain = jnp.sum(grad_first * normed_one, axis=0)
    grad_norm_bias = jnp.sum(grad_first, axis=0)
    grad_inputs = grad_hidden_in + norm_back(grad_first * norm_gain, normed_one, scale_one)
    input_grad = grad_inputs.reshape(seq_count, block, width)
    row_sums = (
        lax.psum_scatter(grad_out_w, ("dp", "seq"), scatter_dimension=1, tiled=True),
        lax.psum_scatter(grad_down, ("dp", "seq"), scatter_dimension=1, tiled=True),
    )
    column_sums = (
        lax.psum_scatter(grad_norm_gain, ("dp", "seq"), scatter_dimension=0, tiled=True),
        lax.psum_scatter(grad_norm_bias, ("dp", "seq"), scatter_dimension=0, tiled=True),
        lax.psum_scatter(grad_mlp_gain, ("dp", "seq"), scatter_dimension=0, tiled=True),
        lax.psum_scatter(grad_mlp_bias, ("dp", "seq"), scatter_dimension=0, tiled=True),
        lax.psum_scatter(grad_wq, ("dp", "seq"), scatter_dimension=0, tiled=True),
        lax.psum_scatter(grad_wk, ("dp", "seq"), scatter_dimension=0, tiled=True),
        lax.psum_scatter(grad_wv, ("dp", "seq"), scatter_dimension=0, tiled=True),
        lax.psum_scatter(grad_ws, ("dp", "seq"), scatter_dimension=0, tiled=True),
        lax.psum_scatter(grad_gate, ("dp", "seq"), scatter_dimension=0, tiled=True),
        lax.psum_scatter(grad_up, ("dp", "seq"), scatter_dimension=0, tiled=True),
    )
    return (
        mixed_out,
        input_grad,
        column_sums[0],
        column_sums[1],
        column_sums[2],
        column_sums[3],
        column_sums[4],
        column_sums[5],
        column_sums[6],
        column_sums[7],
        row_sums[0],
        column_sums[8],
        column_sums[9],
        row_sums[1],
    )


def solution(mesh):
    return jax.shard_map(
        on_device,
        mesh=mesh,
        in_specs=(
            P("dp", "seq", None),
            P(("dp", "seq")),
            P(("dp", "seq")),
            P(("dp", "seq")),
            P(("dp", "seq")),
            P(("dp", "seq"), "tensor"),
            P(("dp", "seq"), "tensor"),
            P(("dp", "seq"), "tensor"),
            P(("dp", "seq"), "tensor"),
            P("tensor", ("dp", "seq")),
            P(("dp", "seq"), "tensor"),
            P(("dp", "seq"), "tensor"),
            P("tensor", ("dp", "seq")),
            P("tensor"),
            P("dp", "seq", None),
        ),
        out_specs=(
            P("dp", "seq", None),
            P("dp", "seq", None),
            P(("dp", "seq")),
            P(("dp", "seq")),
            P(("dp", "seq")),
            P(("dp", "seq")),
            P(("dp", "seq"), "tensor"),
            P(("dp", "seq"), "tensor"),
            P(("dp", "seq"), "tensor"),
            P(("dp", "seq"), "tensor"),
            P("tensor", ("dp", "seq")),
            P(("dp", "seq"), "tensor"),
            P(("dp", "seq"), "tensor"),
            P("tensor", ("dp", "seq")),
        ),
        check_vma=False,
    )
```

profile of v0, /device:TPU:0, one launch (start us, length us, event | category | flops | bytes accessed | tf_op | source)
XLA Modules:
  0.0 3024.8 jit_solution(7418860865744071854)
XLA Ops:
  10.6 34.2 %all-gather = bf16[16,1,128]{2,1,0:T(2,128)(2,1)S(1)} all-gather(bf16[1,1,128]{2,1,0:T(2,128)(2,1)} %bitcast.195), channel_id=1, replica_groups=mesh['tensor'=2,'dp'=4,'seq'=4] {'dp','seq'}, dimensions={0}, use_global_device_ids=true | all-gather | bytes 4352 | tf_op jit(solution)/shard_map/all_gather | solution.py:86
  132.7 57.1 %all-gather.15.cloned.1.call-done = bf16[2048,2048]{1,0:T(8,128)(2,1)} async-done(((bf16[128,2048]{1,0:T(8,128)(2,1)}), bf16[2048,2048]{1,0:T(8,128)(2,1)}) %all-gather.15.cloned.1.call-update) | async-done | bytes 8388624 | tf_op jit(solution)/shard_map/all_gather | solution.py:92
  214.2 374.2 %while.24 = (s32[]{:T(128)}, f32[2,4,256,512]{3,2,1,0:T(8,128)}, f32[2,4,256,512]{3,2,1,0:T(8,128)}, f32[4]{0:T(128)S(1)}, f32[2,4,256,512]{3,2,1,0:T(8,128)}, /*index=5*/s32[]{:T(128)}) while((s32[]{:T(128)}, f32[2,4,256,512]{3,2,1,0:T(8,128)}, f32[2,4,256,512]{3,2,1,0:T(8,128)}, f32[4]{0:T(128)S(1)}, f32[2,4,256,512]{3,2,1,0:T(8,128)}, ...), condition=%wide.region_3.4_spmd, body=%wide.region_2.3_spmd.sunk | while | flops 2097154 | bytes 29360252 | solution.py:136
  219.7 154.2 %collective-permute-done = f32[2,4,256,512]{3,2,1,0:T(8,128)} collective-permute-done((f32[2,4,256,512]{3,2,1,0:T(8,128)}, f32[2,4,256,512]{3,2,1,0:T(8,128)}, u32[]{:S(2)}, u32[]{:S(2)}) %collective-permute-start) | collective-permute-done | bytes 4194336 | tf_op jit(solution)/shard_map/while/body/eval_jaxpr/ppermute | solution.py:15
  390.0 92.2 %collective-permute-done = f32[2,4,256,512]{3,2,1,0:T(8,128)} collective-permute-done((f32[2,4,256,512]{3,2,1,0:T(8,128)}, f32[2,4,256,512]{3,2,1,0:T(8,128)}, u32[]{:S(2)}, u32[]{:S(2)}) %collective-permute-start) | collective-permute-done | bytes 4194336 | tf_op jit(solution)/shard_map/while/body/eval_jaxpr/ppermute | solution.py:15
  495.3 86.5 %collective-permute-done = f32[2,4,256,512]{3,2,1,0:T(8,128)} collective-permute-done((f32[2,4,256,512]{3,2,1,0:T(8,128)}, f32[2,4,256,512]{3,2,1,0:T(8,128)}, u32[]{:S(2)}, u32[]{:S(2)}) %collective-permute-start) | collective-permute-done | bytes 4194336 | tf_op jit(solution)/shard_map/while/body/eval_jaxpr/ppermute | solution.py:15
  701.4 46.9 %all-reduce.10.cloned.1.call-done = f32[512,2048]{1,0:T(8,128)} async-done(((f32[512,2048]{1,0:T(8,128)}), f32[512,2048]{1,0:T(8,128)}) %all-reduce.10.cloned.1.call-update) | async-done | bytes 4194320 | tf_op jit(solution)/shard_map/psum | solution.py:147
  753.9 71.0 %all-gather.23.cloned.1.call-done = bf16[2048,2048]{1,0:T(8,128)(2,1)} async-done(((bf16[128,2048]{1,0:T(8,128)(2,1)}), bf16[2048,2048]{1,0:T(8,128)(2,1)}) %all-gather.23.cloned.1.call-update) | async-done | bytes 8388624 | tf_op jit(solution)/shard_map/all_gather | solution.py:94
  834.7 65.3 %all-gather.25.cloned.1.call-done = bf16[2048,2048]{1,0:T(8,128)(2,1)} async-done(((bf16[128,2048]{1,0:T(8,128)(2,1)}), bf16[2048,2048]{1,0:T(8,128)(2,1)}) %all-gather.25.cloned.1.call-update) | async-done | bytes 8388624 | tf_op jit(solution)/shard_map/all_gather | solution.py:95
  909.4 69.0 %all-gather.27.cloned.1.call-done = bf16[2048,2048]{1,0:T(8,128)(2,1)} async-done(((bf16[2048,128]{1,0:T(8,128)(2,1)}), bf16[2048,2048]{1,0:T(8,128)(2,1)}) %all-gather.27.cloned.1.call-update) | async-done | bytes 8388624 | tf_op jit(solution)/shard_map/all_gather | solution.py:104
  1015.5 96.9 %all-reduce.14.cloned.1.call-done = f32[512,2048]{1,0:T(8,128)} async-done(((f32[512,2048]{1,0:T(8,128)}), f32[512,2048]{1,0:T(8,128)}) %all-reduce.14.cloned.1.call-update) | async-done | bytes 4194320 | tf_op jit(solution)/shard_map/psum | solution.py:170
  1117.4 60.9 %all-reduce.12.cloned.1.call-done = bf16[512,2048]{1,0:T(8,128)(2,1)} async-done(((bf16[512,2048]{1,0:T(8,128)(2,1)}), bf16[512,2048]{1,0:T(8,128)(2,1)}) %all-reduce.12.cloned.1.call-update) | async-done | bytes 2097168 | tf_op jit(solution)/shard_map/psum | solution.py:155
  1239.9 300.7 %while.25 = (s32[]{:T(128)}, f32[2,4,256,512]{3,2,1,0:T(8,128)}, f32[2,4,256,512]{3,2,1,0:T(8,128)}, f32[4]{0:T(128)S(1)}, f32[2,4,256,512]{3,2,1,0:T(8,128)}, /*index=5*/s32[]{:T(128)}) while((s32[]{:T(128)}, f32[2,4,256,512]{3,2,1,0:T(8,128)}, f32[2,4,256,512]{3,2,1,0:T(8,128)}, f32[4]{0:T(128)S(1)}, f32[2,4,256,512]{3,2,1,0:T(8,128)}, ...), condition=%wide.region_16.17_spmd, body=%wide.region_15.16_spmd.sunk | while | flops 2097154 | bytes 29360252 | solution.py:205
  1241.3 93.1 %collective-permute-done.1 = f32[2,4,256,512]{3,2,1,0:T(8,128)} collective-permute-done((f32[2,4,256,512]{3,2,1,0:T(8,128)}, f32[2,4,256,512]{3,2,1,0:T(8,128)}, u32[]{:S(2)}, u32[]{:S(2)}) %collective-permute-start.1) | collective-permute-done | bytes 4194336 | tf_op jit(solution)/shard_map/while/body/eval_jaxpr/ppermute | solution.py:15
  1342.2 92.2 %collective-permute-done.1 = f32[2,4,256,512]{3,2,1,0:T(8,128)} collective-permute-done((f32[2,4,256,512]{3,2,1,0:T(8,128)}, f32[2,4,256,512]{3,2,1,0:T(8,128)}, u32[]{:S(2)}, u32[]{:S(2)}) %collective-permute-start.1) | collective-permute-done | bytes 4194336 | tf_op jit(solution)/shard_map/while/body/eval_jaxpr/ppermute | solution.py:15
  1442.3 91.3 %collective-permute-done.1 = f32[2,4,256,512]{3,2,1,0:T(8,128)} collective-permute-done((f32[2,4,256,512]{3,2,1,0:T(8,128)}, f32[2,4,256,512]{3,2,1,0:T(8,128)}, u32[]{:S(2)}, u32[]{:S(2)}) %collective-permute-start.1) | collective-permute-done | bytes 4194336 | tf_op jit(solution)/shard_map/while/body/eval_jaxpr/ppermute | solution.py:15
  1718.3 63.8 %all-reduce.4 = (f32[2048]{0:T(1024)S(1)}, f32[2048]{0:T(1024)S(1)}, f32[2048]{0:T(1024)S(1)}, f32[2048]{0:T(1024)S(1)}) all-reduce(f32[2048]{0:T(1024)S(1)} %get-tuple-element.70, f32[2048]{0:T(1024)S(1)} %get-tuple-element.75, f32[2048]{0:T(1024)S(1)} %copy-done.52, ...), channel_id=2, replica_groups=mesh['tensor'=2,'dp'=4,'seq'=4] {'dp','seq'}, use_global_device_ids=true, to_apply=%region_21.22.clone | all-reduce | flops 8192 | bytes 65536
  1823.8 107.6 %reduce-scatter.9.cloned.1.call-done = f32[128,1024]{1,0:T(8,128)} async-done(((f32[2048,1024]{1,0:T(8,128)}), f32[128,1024]{1,0:T(8,128)}) %reduce-scatter.9.cloned.1.call-update) | async-done | bytes 524304 | tf_op jit(solution)/shard_map/reduce_scatter | solution.py:251
  1931.4 181.6 %reduce-scatter.19.cloned.1.call-done = f32[128,2048]{1,0:T(8,128)} async-done(((f32[2048,2048]{1,0:T(8,128)}), f32[128,2048]{1,0:T(8,128)}) %reduce-scatter.19.cloned.1.call-update) | async-done | bytes 1048592 | tf_op jit(solution)/shard_map/reduce_scatter | solution.py:255
  2113.0 181.0 %reduce-scatter.21.cloned.1.call-done = f32[128,2048]{1,0:T(8,128)} async-done(((f32[2048,2048]{1,0:T(8,128)}), f32[128,2048]{1,0:T(8,128)}) %reduce-scatter.21.cloned.1.call-update) | async-done | bytes 1048592 | tf_op jit(solution)/shard_map/reduce_scatter | solution.py:256
  2294.0 180.8 %reduce-scatter.23.cloned.1.call-done = f32[2048,128]{1,0:T(8,128)} async-done(((f32[2048,2048]{1,0:T(8,128)}), f32[2048,128]{1,0:T(8,128)}) %reduce-scatter.23.cloned.1.call-update) | async-done | bytes 1048592 | tf_op jit(solution)/shard_map/reduce_scatter | solution.py:244
  2474.8 180.8 %reduce-scatter.17.cloned.1.call-done = f32[2048,128]{1,0:T(8,128)} async-done(((f32[2048,2048]{1,0:T(8,128)}), f32[2048,128]{1,0:T(8,128)}) %reduce-scatter.17.cloned.1.call-update) | async-done | bytes 1048592 | tf_op jit(solution)/shard_map/reduce_scatter | solution.py:243
  2655.6 181.2 %reduce-scatter.13.cloned.1.call-done = f32[128,2048]{1,0:T(8,128)} async-done(((f32[2048,2048]{1,0:T(8,128)}), f32[128,2048]{1,0:T(8,128)}) %reduce-scatter.13.cloned.1.call-update) | async-done | bytes 1048592 | tf_op jit(solution)/shard_map/reduce_scatter | solution.py:253
  2836.7 181.0 %reduce-scatter.15.cloned.1.call-done = f32[128,2048]{1,0:T(8,128)} async-done(((f32[2048,2048]{1,0:T(8,128)}), f32[128,2048]{1,0:T(8,128)}) %reduce-scatter.15.cloned.1.call-update) | async-done | bytes 1048592 | tf_op jit(solution)/shard_map/reduce_scatter | solution.py:254
  (301 shorter events, 639.8 us)
Async XLA Ops:
  7.9 106.8 %all-gather.17.cloned.1.call-start = ((), (), s32[]{:S(2)}) async-start(), calls=%async_computation.10 | async-start | bytes 4456448 | tf_op jit(solution)/shard_map/all_gather | solution.py:90
  8.7 181.1 %all-gather.15.cloned.1.call-start = ((), (), s32[]{:S(2)}) async-start(), calls=%async_computation.9 | async-start | bytes 8912896 | tf_op jit(solution)/shard_map/all_gather | solution.py:92
  9.4 605.3 %all-gather.13.cloned.1.call-start = ((), (), s32[]{:S(2)}) async-start(), calls=%async_computation.8 | async-start | bytes 8912896 | tf_op jit(solution)/shard_map/all_gather | solution.py:93
  10.0 617.6 %all-gather.21.cloned.1.call-start = ((), (), s32[]{:S(2)}) async-start(), calls=%async_computation.12 | async-start | bytes 8912896 | tf_op jit(solution)/shard_map/all_gather | solution.py:103
  10.6 737.8 %all-reduce.10.cloned.1.call-start = ((), (), s32[]{:S(2)}) async-start(), calls=%async_computation.13 | async-start | bytes 8388608 | tf_op jit(solution)/shard_map/psum | solution.py:147
  214.2 159.7 %collective-permute-start = (f32[2,4,256,512]{3,2,1,0:T(8,128)}, f32[2,4,256,512]{3,2,1,0:T(8,128)}, u32[]{:S(2)}, u32[]{:S(2)}) collective-permute-start(f32[2,4,256,512]{3,2,1,0:T(8,128)} %get-tuple-element.204), channel_id=1, source_target_pairs={{0,1},{1,2},{2,3},{4,5},{5,6},{6,7},{8,9},{9,10},{10,11},{12,13},{... | collective-permute-start | bytes 12582920 | tf_op jit(solution)/shard_map/while/body/eval_jaxpr/ppermute | solution.py:15
  380.5 101.7 %collective-permute-start = (f32[2,4,256,512]{3,2,1,0:T(8,128)}, f32[2,4,256,512]{3,2,1,0:T(8,128)}, u32[]{:S(2)}, u32[]{:S(2)}) collective-permute-start(f32[2,4,256,512]{3,2,1,0:T(8,128)} %get-tuple-element.204), channel_id=1, source_target_pairs={{0,1},{1,2},{2,3},{4,5},{5,6},{6,7},{8,9},{9,10},{10,11},{12,13},{... | collective-permute-start | bytes 12582920 | tf_op jit(solution)/shard_map/while/body/eval_jaxpr/ppermute | solution.py:15
  488.8 93.0 %collective-permute-start = (f32[2,4,256,512]{3,2,1,0:T(8,128)}, f32[2,4,256,512]{3,2,1,0:T(8,128)}, u32[]{:S(2)}, u32[]{:S(2)}) collective-permute-start(f32[2,4,256,512]{3,2,1,0:T(8,128)} %get-tuple-element.204), channel_id=1, source_target_pairs={{0,1},{1,2},{2,3},{4,5},{5,6},{6,7},{8,9},{9,10},{10,11},{12,13},{... | collective-permute-start | bytes 12582920 | tf_op jit(solution)/shard_map/while/body/eval_jaxpr/ppermute | solution.py:15
  638.2 186.7 %all-gather.23.cloned.1.call-start = ((), (), s32[]{:S(2)}) async-start(), calls=%async_computation.14 | async-start | bytes 8912896 | tf_op jit(solution)/shard_map/all_gather | solution.py:94
  638.9 261.1 %all-gather.25.cloned.1.call-start = ((), (), s32[]{:S(2)}) async-start(), calls=%async_computation.15 | async-start | bytes 8912896 | tf_op jit(solution)/shard_map/all_gather | solution.py:95
  639.7 338.8 %all-gather.27.cloned.1.call-start = ((), (), s32[]{:S(2)}) async-start(), calls=%async_computation.16 | async-start | bytes 8912896 | tf_op jit(solution)/shard_map/all_gather | solution.py:104
  640.4 472.0 %all-reduce.14.cloned.1.call-start = ((), (), s32[]{:S(2)}) async-start(), calls=%async_computation.18 | async-start | bytes 8388608 | tf_op jit(solution)/shard_map/psum | solution.py:170
  1006.1 172.1 %all-reduce.12.cloned.1.call-start = ((), (), s32[]{:S(2)}) async-start(), calls=%async_computation.17 | async-start | bytes 4194304 | tf_op jit(solution)/shard_map/psum | solution.py:155
  1015.5 699.1 %all-reduce.16.cloned.1.call-start = ((), (), s32[]{:S(2)}) async-start(), calls=%async_computation.19 | async-start | bytes 8388608 | tf_op jit(solution)/shard_map/psum | solution.py:237
  1239.9 94.5 %collective-permute-start.1 = (f32[2,4,256,512]{3,2,1,0:T(8,128)}, f32[2,4,256,512]{3,2,1,0:T(8,128)}, u32[]{:S(2)}, u32[]{:S(2)}) collective-permute-start(f32[2,4,256,512]{3,2,1,0:T(8,128)} %get-tuple-element.222), channel_id=1, source_target_pairs={{1,0},{2,1},{3,2},{5,4},{6,5},{7,6},{9,8},{10,9},{11,10},{13,12},{... | collective-permute-start | bytes 12582920 | tf_op jit(solution)/shard_map/while/body/eval_jaxpr/ppermute | solution.py:15
  1340.9 93.5 %collective-permute-start.1 = (f32[2,4,256,512]{3,2,1,0:T(8,128)}, f32[2,4,256,512]{3,2,1,0:T(8,128)}, u32[]{:S(2)}, u32[]{:S(2)}) collective-permute-start(f32[2,4,256,512]{3,2,1,0:T(8,128)} %get-tuple-element.222), channel_id=1, source_target_pairs={{1,0},{2,1},{3,2},{5,4},{6,5},{7,6},{9,8},{10,9},{11,10},{13,12},{... | collective-permute-start | bytes 12582920 | tf_op jit(solution)/shard_map/while/body/eval_jaxpr/ppermute | solution.py:15
  1607.4 216.3 %reduce-scatter.11.cloned.1.call-start = ((), (), s32[]{:S(2)}) async-start(), calls=%async_computation.21 | async-start | bytes 8912896 | tf_op jit(solution)/shard_map/reduce_scatter | solution.py:252
  1615.9 315.5 %reduce-scatter.9.cloned.1.call-start = ((), (), s32[]{:S(2)}) async-start(), calls=%async_computation.20 | async-start | bytes 8912896 | tf_op jit(solution)/shard_map/reduce_scatter | solution.py:251
  1621.9 491.1 %reduce-scatter.19.cloned.1.call-start = ((), (), s32[]{:S(2)}) async-start(), calls=%async_computation.25 | async-start | bytes 17825792 | tf_op jit(solution)/shard_map/reduce_scatter | solution.py:255
  1634.6 659.4 %reduce-scatter.21.cloned.1.call-start = ((), (), s32[]{:S(2)}) async-start(), calls=%async_computation.26 | async-start | bytes 17825792 | tf_op jit(solution)/shard_map/reduce_scatter | solution.py:256
  1647.2 827.6 %reduce-scatter.23.cloned.1.call-start = ((), (), s32[]{:S(2)}) async-start(), calls=%async_computation.27 | async-start | bytes 17825792 | tf_op jit(solution)/shard_map/reduce_scatter | solution.py:244
  1660.3 995.3 %reduce-scatter.17.cloned.1.call-start = ((), (), s32[]{:S(2)}) async-start(), calls=%async_computation.24 | async-start | bytes 17825792 | tf_op jit(solution)/shard_map/reduce_scatter | solution.py:243
  1673.8 1163.0 %reduce-scatter.13.cloned.1.call-start = ((), (), s32[]{:S(2)}) async-start(), calls=%async_computation.22 | async-start | bytes 17825792 | tf_op jit(solution)/shard_map/reduce_scatter | solution.py:253
  1684.0 1333.8 %reduce-scatter.15.cloned.1.call-start = ((), (), s32[]{:S(2)}) async-start(), calls=%async_computation.23 | async-start | bytes 17825792 | tf_op jit(solution)/shard_map/reduce_scatter | solution.py:254
  (68 other events, 2201.5 us)
Sparse Core Ops, SparseCore 0:
  10.2 53.3 all-gather.18
  65.8 48.8 all-gather.16
  116.9 72.8 all-gather.14
  191.8 99.6 all-gather.12
  293.5 105.5 all-gather.20
  638.3 110.0 all-reduce.9
  750.6 74.2 all-gather.22
  827.1 72.8 all-gather.24
  902.1 76.2 all-gather.26
  1006.3 106.0 all-reduce.13
  1115.3 62.9 all-reduce.11
  1607.6 106.9 all-reduce.15
  1719.2 104.4 reduce-scatter.10
  1828.3 103.0 reduce-scatter.8
  1935.9 176.9 reduce-scatter.18
  2117.5 176.4 reduce-scatter.20
  2298.5 176.2 reduce-scatter.22
  2479.3 176.2 reduce-scatter.16
  2660.3 176.4 reduce-scatter.12
  2841.3 176.4 reduce-scatter.14
where the time goes:
time: 3030 us; the launch traced here: 3020 us
  waiting for transfers between devices  2350 us (78%)
  matrix products  271 us (9%)
  blocking collectives  188 us (6%)
  other arithmetic  92.2 us (3%)
  local copies, waits for them, and re-layouts  78.8 us (3%)
    ppermute x6, waiting for transfers between devices, passed_along(): return lax.ppermute(x, axis, pairs)  610 us
    reduce_scatter x1, waiting for transfers between devices, on_device(): lax.psum_scatter(grad_gate, ('dp', 'seq'), scatter_dimension=0, tiled=True)  182 us
    reduce_scatter x1, waiting for transfers between devices, on_device(): lax.psum_scatter(grad_wv, ('dp', 'seq'), scatter_dimension=0, tiled=True)  181 us
    reduce_scatter x1, waiting for transfers between devices, on_device(): lax.psum_scatter(grad_up, ('dp', 'seq'), scatter_dimension=0, tiled=True)  181 us
    reduce_scatter x1, waiting for transfers between devices, on_device(): lax.psum_scatter(grad_ws, ('dp', 'seq'), scatter_dimension=0, tiled=True)  181 us
    reduce_scatter x1, waiting for transfers between devices, on_device(): lax.psum_scatter(grad_out_w, ('dp', 'seq'), scatter_dimension=1, tiled=True)  181 us
    reduce_scatter x1, waiting for transfers between devices, on_device(): lax.psum_scatter(grad_down, ('dp', 'seq'), scatter_dimension=1, tiled=True)  181 us
    reduce_scatter x1, waiting for transfers between devices, on_device(): lax.psum_scatter(grad_wq, ('dp', 'seq'), scatter_dimension=0, tiled=True)  108 us
  transfers between devices with their start and end apart: 26, of which 23 were waited for; matrix products, arithmetic and copies ran while one was open for 8% of the time, Pallas kernels for 0%

commit v1 on v0

--- a/solution.py
+++ b/solution.py
@@ -7,6 +7,18 @@
 VH = 512
 eps = 1e-05
 highest_precision = lax.Precision.HIGHEST
+
+
+def doubled_up(array, axis, dim):
+    ways, here, hop = (lax.axis_size(axis), lax.axis_index(axis), array.shape[dim])
+    line, have = (array, 1)
+    while have < ways:
+        line = jnp.concatenate(
+            [line, lax.ppermute(line, axis, [(d, (d - have) % ways) for d in range(ways)])],
+            axis=dim,
+        )
+        have = 2 * have
+    return jnp.roll(line, here * hop, axis=dim)
 
 
 def passed_along(x, axis, by):
@@ -101,7 +113,7 @@
     query_full, key_full, value_full, swish_full, gate_full, up_full = gathered[4:]
     out_full, down_full = (
         lax.all_gather(w_out, ("dp", "seq"), axis=1, tiled=True),
-        lax.all_gather(w_down, ("dp", "seq"), axis=1, tiled=True),
+        doubled_up(w_down, ("dp", "seq"), 1),
     )
     seq_count, block, width = tokens.shape
     row_count = seq_count * block

time: 3030 us -> 2990 us (0.987)
  waiting for transfers between devices: 2350 us -> 2280 us
    ppermute x0 -> x4, waiting for transfers between devices: none -> 136 us  [doubled_up(): lax.ppermute(line, axis, [(d, (d - have) % ways) for d in range(ways)])]
    all_gather x1, waiting for transfers between devices: 71 us -> 0.02 us  [on_device(): lax.all_gather(w_gate, ('dp', 'seq'), axis=0, tiled=True)]
    all_gather x1 -> x0, waiting for transfers between devices: 69 us -> none  [on_device(): lax.all_gather(w_down, ('dp', 'seq'), axis=1, tiled=True)]
    psum x1, waiting for transfers between devices: 46.9 us -> 0.01 us  [on_device(): attention = lax.psum(matmul(mixed, out_full), 'tensor')]
  transfers between devices with their start and end apart: 26 -> 29, of which waited for: 23 -> 24; matrix products, arithmetic and copies ran while one was open for 8% -> 9% of each run, Pallas kernels for 0% -> 0%
where the time goes in v1:
time: 2990 us
  waiting for transfers between devices  2280 us (76%)
  matrix products  275 us (9%)
  blocking collectives  188 us (6%)
  local copies, waits for them, and re-layouts  99.2 us (3%)
  other arithmetic  97.1 us (3%)
  starting transfers between devices  33 us (1%)
    ppermute x6, waiting for transfers between devices, passed_along(): return lax.ppermute(x, axis, pairs)  609 us
    reduce_scatter x1, waiting for transfers between devices, on_device(): lax.psum_scatter(grad_gate, ('dp', 'seq'), scatter_dimension=0, tiled=True)  182 us
    reduce_scatter x1, waiting for transfers between devices, on_device(): lax.psum_scatter(grad_ws, ('dp', 'seq'), scatter_dimension=0, tiled=True)  181 us
    reduce_scatter x1, waiting for transfers between devices, on_device(): lax.psum_scatter(grad_wv, ('dp', 'seq'), scatter_dimension=0, tiled=True)  181 us
    reduce_scatter x1, waiting for transfers between devices, on_device(): lax.psum_scatter(grad_up, ('dp', 'seq'), scatter_dimension=0, tiled=True)  181 us
    reduce_scatter x1, waiting for transfers between devices, on_device(): lax.psum_scatter(grad_down, ('dp', 'seq'), scatter_dimension=1, tiled=True)  181 us
    reduce_scatter x1, waiting for transfers between devices, on_device(): lax.psum_scatter(grad_out_w, ('dp', 'seq'), scatter_dimension=1, tiled=True)  181 us
    ppermute x4, waiting for transfers between devices, doubled_up(): lax.ppermute(line, axis, [(d, (d - have) % ways) for d in range(ways)])  136 us
  transfers between devices with their start and end apart: 29, of which 24 were waited for; matrix products, arithmetic and copies ran while one was open for 9% of the time, Pallas kernels for 0%

profile of v1, /device:TPU:0, one launch (start us, length us, event | category | flops | bytes accessed | tf_op | source)
XLA Modules:
  0.0 2985.4 jit_solution(7609215481057859809)
XLA Ops:
  10.6 34.2 %all-gather = bf16[16,1,128]{2,1,0:T(2,128)(2,1)S(1)} all-gather(bf16[1,1,128]{2,1,0:T(2,128)(2,1)} %bitcast.200), channel_id=1, replica_groups=mesh['tensor'=2,'dp'=4,'seq'=4] {'dp','seq'}, dimensions={0}, use_global_device_ids=true | all-gather | bytes 4352 | tf_op jit(solution)/shard_map/all_gather | solution.py:98
  132.7 57.1 %all-gather.14.cloned.1.call-done = bf16[2048,2048]{1,0:T(8,128)(2,1)} async-done(((bf16[128,2048]{1,0:T(8,128)(2,1)}), bf16[2048,2048]{1,0:T(8,128)(2,1)}) %all-gather.14.cloned.1.call-update) | async-done | bytes 8388624 | tf_op jit(solution)/shard_map/all_gather | solution.py:104
  214.2 374.3 %while.24 = (s32[]{:T(128)}, f32[2,4,256,512]{3,2,1,0:T(8,128)}, f32[2,4,256,512]{3,2,1,0:T(8,128)}, f32[4]{0:T(128)S(1)}, f32[2,4,256,512]{3,2,1,0:T(8,128)}, /*index=5*/s32[]{:T(128)}) while((s32[]{:T(128)}, f32[2,4,256,512]{3,2,1,0:T(8,128)}, f32[2,4,256,512]{3,2,1,0:T(8,128)}, f32[4]{0:T(128)S(1)}, f32[2,4,256,512]{3,2,1,0:T(8,128)}, ...), condition=%wide.region_3.4_spmd, body=%wide.region_2.3_spmd.sunk | while | flops 2097154 | bytes 29360252 | solution.py:148
  219.7 154.2 %collective-permute-done = f32[2,4,256,512]{3,2,1,0:T(8,128)} collective-permute-done((f32[2,4,256,512]{3,2,1,0:T(8,128)}, f32[2,4,256,512]{3,2,1,0:T(8,128)}, u32[]{:S(2)}, u32[]{:S(2)}) %collective-permute-start) | collective-permute-done | bytes 4194336 | tf_op jit(solution)/shard_map/while/body/eval_jaxpr/ppermute | solution.py:27
  390.1 92.1 %collective-permute-done = f32[2,4,256,512]{3,2,1,0:T(8,128)} collective-permute-done((f32[2,4,256,512]{3,2,1,0:T(8,128)}, f32[2,4,256,512]{3,2,1,0:T(8,128)}, u32[]{:S(2)}, u32[]{:S(2)}) %collective-permute-start) | collective-permute-done | bytes 4194336 | tf_op jit(solution)/shard_map/while/body/eval_jaxpr/ppermute | solution.py:27
  495.4 86.5 %collective-permute-done = f32[2,4,256,512]{3,2,1,0:T(8,128)} collective-permute-done((f32[2,4,256,512]{3,2,1,0:T(8,128)}, f32[2,4,256,512]{3,2,1,0:T(8,128)}, u32[]{:S(2)}, u32[]{:S(2)}) %collective-permute-start) | collective-permute-done | bytes 4194336 | tf_op jit(solution)/shard_map/while/body/eval_jaxpr/ppermute | solution.py:27
  656.4 48.5 %collective-permute-done.3 = bf16[2048,256]{1,0:T(8,128)(2,1)S(1)} collective-permute-done((bf16[2048,256]{1,0:T(8,128)(2,1)S(1)}, bf16[2048,256]{1,0:T(8,128)(2,1)S(1)}, u32[]{:S(2)}, u32[]{:S(2)}) %collective-permute-start.3) | collective-permute-done | bytes 1048608 | tf_op jit(solution)/shard_map/ppermute | solution.py:17
  802.2 52.2 %collective-permute-done.5 = bf16[2048,1024]{1,0:T(8,128)(2,1)} collective-permute-done((bf16[2048,1024]{1,0:T(8,128)(2,1)}, bf16[2048,1024]{1,0:T(8,128)(2,1)}, u32[]{:S(2)}, u32[]{:S(2)}) %collective-permute-start.5) | collective-permute-done | bytes 4194336 | tf_op jit(solution)/shard_map/ppermute | solution.py:17
  883.7 42.2 %all-gather.24.cloned.1.call-done = bf16[2048,2048]{1,0:T(8,128)(2,1)} async-done(((bf16[128,2048]{1,0:T(8,128)(2,1)}), bf16[2048,2048]{1,0:T(8,128)(2,1)}) %all-gather.24.cloned.1.call-update) | async-done | bytes 8388624 | tf_op jit(solution)/shard_map/all_gather | solution.py:107
  976.1 97.3 %all-reduce.14.cloned.1.call-done = f32[512,2048]{1,0:T(8,128)} async-done(((f32[512,2048]{1,0:T(8,128)}), f32[512,2048]{1,0:T(8,128)}) %all-reduce.14.cloned.1.call-update) | async-done | bytes 4194320 | tf_op jit(solution)/shard_map/psum | solution.py:182
  1078.4 60.7 %all-reduce.12.cloned.1.call-done = bf16[512,2048]{1,0:T(8,128)(2,1)} async-done(((bf16[512,2048]{1,0:T(8,128)(2,1)}), bf16[512,2048]{1,0:T(8,128)(2,1)}) %all-reduce.12.cloned.1.call-update) | async-done | bytes 2097168 | tf_op jit(solution)/shard_map/psum | solution.py:167
  1200.9 300.5 %while.25 = (s32[]{:T(128)}, f32[2,4,256,512]{3,2,1,0:T(8,128)}, f32[2,4,256,512]{3,2,1,0:T(8,128)}, f32[4]{0:T(128)S(1)}, f32[2,4,256,512]{3,2,1,0:T(8,128)}, /*index=5*/s32[]{:T(128)}) while((s32[]{:T(128)}, f32[2,4,256,512]{3,2,1,0:T(8,128)}, f32[2,4,256,512]{3,2,1,0:T(8,128)}, f32[4]{0:T(128)S(1)}, f32[2,4,256,512]{3,2,1,0:T(8,128)}, ...), condition=%wide.region_16.17_spmd, body=%wide.region_15.16_spmd.sunk | while | flops 2097154 | bytes 29360252 | solution.py:217
  1202.4 93.1 %collective-permute-done.1 = f32[2,4,256,512]{3,2,1,0:T(8,128)} collective-permute-done((f32[2,4,256,512]{3,2,1,0:T(8,128)}, f32[2,4,256,512]{3,2,1,0:T(8,128)}, u32[]{:S(2)}, u32[]{:S(2)}) %collective-permute-start.1) | collective-permute-done | bytes 4194336 | tf_op jit(solution)/shard_map/while/body/eval_jaxpr/ppermute | solution.py:27
  1303.3 92.2 %collective-permute-done.1 = f32[2,4,256,512]{3,2,1,0:T(8,128)} collective-permute-done((f32[2,4,256,512]{3,2,1,0:T(8,128)}, f32[2,4,256,512]{3,2,1,0:T(8,128)}, u32[]{:S(2)}, u32[]{:S(2)}) %collective-permute-start.1) | collective-permute-done | bytes 4194336 | tf_op jit(solution)/shard_map/while/body/eval_jaxpr/ppermute | solution.py:27
  1403.3 91.3 %collective-permute-done.1 = f32[2,4,256,512]{3,2,1,0:T(8,128)} collective-permute-done((f32[2,4,256,512]{3,2,1,0:T(8,128)}, f32[2,4,256,512]{3,2,1,0:T(8,128)}, u32[]{:S(2)}, u32[]{:S(2)}) %collective-permute-start.1) | collective-permute-done | bytes 4194336 | tf_op jit(solution)/shard_map/while/body/eval_jaxpr/ppermute | solution.py:27
  1679.1 63.9 %all-reduce.4 = (f32[2048]{0:T(1024)S(1)}, f32[2048]{0:T(1024)S(1)}, f32[2048]{0:T(1024)S(1)}, f32[2048]{0:T(1024)S(1)}) all-reduce(f32[2048]{0:T(1024)S(1)} %get-tuple-element.70, f32[2048]{0:T(1024)S(1)} %get-tuple-element.75, f32[2048]{0:T(1024)S(1)} %copy-done.61, ...), channel_id=2, replica_groups=mesh['tensor'=2,'dp'=4,'seq'=4] {'dp','seq'}, use_global_device_ids=true, to_apply=%region_21.22.clone | all-reduce | flops 8192 | bytes 65536
  1751.1 33.4 %reduce-scatter.11.cloned.1.call-done = f32[128,1024]{1,0:T(8,128)} async-done(((f32[2048,1024]{1,0:T(8,128)}), f32[128,1024]{1,0:T(8,128)}) %reduce-scatter.11.cloned.1.call-update) | async-done | bytes 524304 | tf_op jit(solution)/shard_map/reduce_scatter | solution.py:264
  1784.5 107.8 %reduce-scatter.9.cloned.1.call-done = f32[128,1024]{1,0:T(8,128)} async-done(((f32[2048,1024]{1,0:T(8,128)}), f32[128,1024]{1,0:T(8,128)}) %reduce-scatter.9.cloned.1.call-update) | async-done | bytes 524304 | tf_op jit(solution)/shard_map/reduce_scatter | solution.py:263
  1892.3 181.5 %reduce-scatter.19.cloned.1.call-done = f32[128,2048]{1,0:T(8,128)} async-done(((f32[2048,2048]{1,0:T(8,128)}), f32[128,2048]{1,0:T(8,128)}) %reduce-scatter.19.cloned.1.call-update) | async-done | bytes 1048592 | tf_op jit(solution)/shard_map/reduce_scatter | solution.py:267
  2073.8 181.0 %reduce-scatter.21.cloned.1.call-done = f32[128,2048]{1,0:T(8,128)} async-done(((f32[2048,2048]{1,0:T(8,128)}), f32[128,2048]{1,0:T(8,128)}) %reduce-scatter.21.cloned.1.call-update) | async-done | bytes 1048592 | tf_op jit(solution)/shard_map/reduce_scatter | solution.py:268
  2254.8 180.8 %reduce-scatter.23.cloned.1.call-done = f32[2048,128]{1,0:T(8,128)} async-done(((f32[2048,2048]{1,0:T(8,128)}), f32[2048,128]{1,0:T(8,128)}) %reduce-scatter.23.cloned.1.call-update) | async-done | bytes 1048592 | tf_op jit(solution)/shard_map/reduce_scatter | solution.py:256
  2435.6 180.8 %reduce-scatter.17.cloned.1.call-done = f32[2048,128]{1,0:T(8,128)} async-done(((f32[2048,2048]{1,0:T(8,128)}), f32[2048,128]{1,0:T(8,128)}) %reduce-scatter.17.cloned.1.call-update) | async-done | bytes 1048592 | tf_op jit(solution)/shard_map/reduce_scatter | solution.py:255
  2616.4 181.0 %reduce-scatter.13.cloned.1.call-done = f32[128,2048]{1,0:T(8,128)} async-done(((f32[2048,2048]{1,0:T(8,128)}), f32[128,2048]{1,0:T(8,128)}) %reduce-scatter.13.cloned.1.call-update) | async-done | bytes 1048592 | tf_op jit(solution)/shard_map/reduce_scatter | solution.py:265
  2797.5 181.1 %reduce-scatter.15.cloned.1.call-done = f32[128,2048]{1,0:T(8,128)} async-done(((f32[2048,2048]{1,0:T(8,128)}), f32[128,2048]{1,0:T(8,128)}) %reduce-scatter.15.cloned.1.call-update) | async-done | bytes 1048592 | tf_op jit(solution)/shard_map/reduce_scatter | solution.py:266
  (341 shorter events, 676.5 us)
Async XLA Ops:
  7.9 106.8 %all-gather.16.cloned.1.call-start = ((), (), s32[]{:S(2)}) async-start(), calls=%async_computation.10 | async-start | bytes 4456448 | tf_op jit(solution)/shard_map/all_gather | solution.py:102
  8.7 181.1 %all-gather.14.cloned.1.call-start = ((), (), s32[]{:S(2)}) async-start(), calls=%async_computation.9 | async-start | bytes 8912896 | tf_op jit(solution)/shard_map/all_gather | solution.py:104
  9.4 605.7 %all-gather.12.cloned.1.call-start = ((), (), s32[]{:S(2)}) async-start(), calls=%async_computation.8 | async-start | bytes 8912896 | tf_op jit(solution)/shard_map/all_gather | solution.py:105
  10.0 617.8 %all-gather.20.cloned.1.call-start = ((), (), s32[]{:S(2)}) async-start(), calls=%async_computation.12 | async-start | bytes 8912896 | tf_op jit(solution)/shard_map/all_gather | solution.py:115
  10.6 857.3 %all-reduce.10.cloned.1.call-start = ((), (), s32[]{:S(2)}) async-start(), calls=%async_computation.13 | async-start | bytes 8388608 | tf_op jit(solution)/shard_map/psum | solution.py:159
  214.2 159.7 %collective-permute-start = (f32[2,4,256,512]{3,2,1,0:T(8,128)}, f32[2,4,256,512]{3,2,1,0:T(8,128)}, u32[]{:S(2)}, u32[]{:S(2)}) collective-permute-start(f32[2,4,256,512]{3,2,1,0:T(8,128)} %get-tuple-element.204), channel_id=1, source_target_pairs={{0,1},{1,2},{2,3},{4,5},{5,6},{6,7},{8,9},{9,10},{10,11},{12,13},{... | collective-permute-start | bytes 12582920 | tf_op jit(solution)/shard_map/while/body/eval_jaxpr/ppermute | solution.py:27
  380.5 101.7 %collective-permute-start = (f32[2,4,256,512]{3,2,1,0:T(8,128)}, f32[2,4,256,512]{3,2,1,0:T(8,128)}, u32[]{:S(2)}, u32[]{:S(2)}) collective-permute-start(f32[2,4,256,512]{3,2,1,0:T(8,128)} %get-tuple-element.204), channel_id=1, source_target_pairs={{0,1},{1,2},{2,3},{4,5},{5,6},{6,7},{8,9},{9,10},{10,11},{12,13},{... | collective-permute-start | bytes 12582920 | tf_op jit(solution)/shard_map/while/body/eval_jaxpr/ppermute | solution.py:27
  488.9 93.0 %collective-permute-start = (f32[2,4,256,512]{3,2,1,0:T(8,128)}, f32[2,4,256,512]{3,2,1,0:T(8,128)}, u32[]{:S(2)}, u32[]{:S(2)}) collective-permute-start(f32[2,4,256,512]{3,2,1,0:T(8,128)} %get-tuple-element.204), channel_id=1, source_target_pairs={{0,1},{1,2},{2,3},{4,5},{5,6},{6,7},{8,9},{9,10},{10,11},{12,13},{... | collective-permute-start | bytes 12582920 | tf_op jit(solution)/shard_map/while/body/eval_jaxpr/ppermute | solution.py:27
  638.3 235.3 %all-gather.22.cloned.1.call-start = ((), (), s32[]{:S(2)}) async-start(), calls=%async_computation.14 | async-start | bytes 8912896 | tf_op jit(solution)/shard_map/all_gather | solution.py:106
  639.1 286.8 %all-gather.24.cloned.1.call-start = ((), (), s32[]{:S(2)}) async-start(), calls=%async_computation.15 | async-start | bytes 8912896 | tf_op jit(solution)/shard_map/all_gather | solution.py:107
  639.8 433.5 %all-reduce.14.cloned.1.call-start = ((), (), s32[]{:S(2)}) async-start(), calls=%async_computation.17 | async-start | bytes 8388608 | tf_op jit(solution)/shard_map/psum | solution.py:182
  733.2 121.1 %collective-permute-start.5 = (bf16[2048,1024]{1,0:T(8,128)(2,1)}, bf16[2048,1024]{1,0:T(8,128)(2,1)}, u32[]{:S(2)}, u32[]{:S(2)}) collective-permute-start(bf16[2048,1024]{1,0:T(8,128)(2,1)} %pad_maximum_fusion), channel_id=1, source_target_pairs={{0,8},{1,9},{2,10},{3,11},{4,12},{5,13},{6,14},{7,15},{8,0},{9,1},... | collective-permute-start | bytes 12582920 | tf_op jit(solution)/shard_map/ppermute | solution.py:17
  966.7 172.4 %all-reduce.12.cloned.1.call-start = ((), (), s32[]{:S(2)}) async-start(), calls=%async_computation.16 | async-start | bytes 4194304 | tf_op jit(solution)/shard_map/psum | solution.py:167
  976.1 699.4 %all-reduce.16.cloned.1.call-start = ((), (), s32[]{:S(2)}) async-start(), calls=%async_computation.18 | async-start | bytes 8388608 | tf_op jit(solution)/shard_map/psum | solution.py:249
  1200.9 94.5 %collective-permute-start.1 = (f32[2,4,256,512]{3,2,1,0:T(8,128)}, f32[2,4,256,512]{3,2,1,0:T(8,128)}, u32[]{:S(2)}, u32[]{:S(2)}) collective-permute-start(f32[2,4,256,512]{3,2,1,0:T(8,128)} %get-tuple-element.222), channel_id=1, source_target_pairs={{1,0},{2,1},{3,2},{5,4},{6,5},{7,6},{9,8},{10,9},{11,10},{13,12},{... | collective-permute-start | bytes 12582920 | tf_op jit(solution)/shard_map/while/body/eval_jaxpr/ppermute | solution.py:27
  1302.0 93.5 %collective-permute-start.1 = (f32[2,4,256,512]{3,2,1,0:T(8,128)}, f32[2,4,256,512]{3,2,1,0:T(8,128)}, u32[]{:S(2)}, u32[]{:S(2)}) collective-permute-start(f32[2,4,256,512]{3,2,1,0:T(8,128)} %get-tuple-element.222), channel_id=1, source_target_pairs={{1,0},{2,1},{3,2},{5,4},{6,5},{7,6},{9,8},{10,9},{11,10},{13,12},{... | collective-permute-start | bytes 12582920 | tf_op jit(solution)/shard_map/while/body/eval_jaxpr/ppermute | solution.py:27
  1568.3 216.2 %reduce-scatter.11.cloned.1.call-start = ((), (), s32[]{:S(2)}) async-start(), calls=%async_computation.20 | async-start | bytes 8912896 | tf_op jit(solution)/shard_map/reduce_scatter | solution.py:264
  1576.8 315.5 %reduce-scatter.9.cloned.1.call-start = ((), (), s32[]{:S(2)}) async-start(), calls=%async_computation.19 | async-start | bytes 8912896 | tf_op jit(solution)/shard_map/reduce_scatter | solution.py:263
  1583.0 490.8 %reduce-scatter.19.cloned.1.call-start = ((), (), s32[]{:S(2)}) async-start(), calls=%async_computation.24 | async-start | bytes 17825792 | tf_op jit(solution)/shard_map/reduce_scatter | solution.py:267
  1595.7 659.1 %reduce-scatter.21.cloned.1.call-start = ((), (), s32[]{:S(2)}) async-start(), calls=%async_computation.25 | async-start | bytes 17825792 | tf_op jit(solution)/shard_map/reduce_scatter | solution.py:268
  1608.3 827.3 %reduce-scatter.23.cloned.1.call-start = ((), (), s32[]{:S(2)}) async-start(), calls=%async_computation.26 | async-start | bytes 17825792 | tf_op jit(solution)/shard_map/reduce_scatter | solution.py:256
  1621.2 995.2 %reduce-scatter.17.cloned.1.call-start = ((), (), s32[]{:S(2)}) async-start(), calls=%async_computation.23 | async-start | bytes 17825792 | tf_op jit(solution)/shard_map/reduce_scatter | solution.py:255
  1634.7 1162.8 %reduce-scatter.13.cloned.1.call-start = ((), (), s32[]{:S(2)}) async-start(), calls=%async_computation.21 | async-start | bytes 17825792 | tf_op jit(solution)/shard_map/reduce_scatter | solution.py:265
  1644.8 1333.7 %reduce-scatter.15.cloned.1.call-start = ((), (), s32[]{:S(2)}) async-start(), calls=%async_computation.22 | async-start | bytes 17825792 | tf_op jit(solution)/shard_map/reduce_scatter | solution.py:266
  (81 other events, 3038.7 us)
Sparse Core Ops, SparseCore 0:
  10.2 53.3 all-gather.17
  65.8 48.8 all-gather.15
  116.9 72.8 all-gather.13
  191.8 99.6 all-gather.11
  293.5 105.5 all-gather.19
  638.5 110.0 all-reduce.9
  750.8 100.1 all-gather.21
  853.2 72.6 all-gather.23
  966.8 106.5 all-reduce.13
  1076.1 62.9 all-reduce.11
  1568.4 106.9 all-reduce.15
  1680.0 104.4 reduce-scatter.10
  1789.1 103.0 reduce-scatter.8
  1896.8 176.9 reduce-scatter.18
  2078.3 176.4 reduce-scatter.20
  2259.3 176.2 reduce-scatter.22
  2440.2 176.2 reduce-scatter.16
  2621.0 176.4 reduce-scatter.12
  2802.1 176.4 reduce-scatter.14
